TPU v7x, 32 devices: a whole 2x2x4 slice. The times are simulated.
32 devices in a mesh: row: 4 (over z), col: 8 (over y, x, core).
Axes of the slice: x: 2, y: 2, z: 4, core: 2. Of those that a mesh axis runs over, the one named last changes fastest.
Arguments:
- factor_wide: float32 [4, 4, 2, 8, 512, 512], P(None, 'row', None, 'col'), may hold values from -1 to 2, as said below
- factor_narrow: bfloat16 [4, 4, 2, 8, 512, 512], P(None, 'row', None, 'col'), may hold values from -1 to 2, as said below
- flags: int32 [4, 4, 2, 8], P(None, 'row', None, 'col'), may hold values from 0 to 1
- forward_solution: float32 [2, 8, 512, 128], P(None, 'col'), may hold values from -0.5 to 0.5
- solution_grad: float32 [2, 8, 512, 128], P(None, 'col'), may hold values from -1.8 to 1.8
Outputs:
- rhs_grad: float32 [4, 4, 512, 128], P(None, 'row')
- factor_grad: float32 [4, 4, 2, 8, 512, 512], P(None, 'row', None, 'col')
Inputs may be any that keep to these rules, and one draw needn't show every extreme that they name: `factor_wide`: the diagonal entries of every diagonal tile lie between 1 and 2. `factor_narrow`: the diagonal entries of every diagonal tile lie between 1 and 2.
All inputs are finite; a program needn't handle non-finite values.
Results may differ from a plain program's by a relative error of at most 0.0003.
Values sent between devices are 32-bit elements; how exact they have to be, the bound alone decides.
A program may use at most 64 MiB of HBM per device.

v0:
```python
import jax
import jax.numpy as jnp
from jax import lax
from jax.sharding import PartitionSpec as P

HIGHEST_PRECISION = lax.Precision.HIGHEST


def broadcast(value, axis, root):
    mine = lax.axis_index(axis) == root
    return lax.psum(jnp.where(mine, value, jnp.zeros_like(value)), axis)


def from_behind(value, axis, by):
    size = lax.axis_size(axis)
    return lax.ppermute(value, axis, [(i, (i + by) % size) for i in range(size)])


def lower_mask(row_index, col_index, tile_width):
    inner_mask = lax.broadcasted_iota(
        jnp.int32, (tile_width, tile_width), 0
    ) >= lax.broadcasted_iota(jnp.int32, (tile_width, tile_width), 1)
    return (row_index > col_index) | (row_index == col_index) & inner_mask


def body(factor_wide, factor_narrow, flags, forward_solution, solution_grad):
    row_count = lax.axis_size("row")
    col_count = lax.axis_size("col")
    my_row = lax.axis_index("row")
    my_col = lax.axis_index("col")
    local_rows = factor_wide.shape[0]
    local_cols = factor_wide.shape[2]
    tile_width = factor_wide.shape[4]
    rhs_width = forward_solution.shape[3]
    tile_count = local_rows * row_count
    factor_tiles = jnp.where(
        flags[:, 0, :, 0, None, None] == 1,
        factor_narrow[:, 0, :, 0].astype(jnp.float32),
        factor_wide[:, 0, :, 0],
    )
    solution_local = forward_solution[:, 0]
    target_local = solution_grad[:, 0]
    row_index = jnp.arange(local_rows, dtype=jnp.int32) * row_count + my_row
    col_index = jnp.arange(local_cols, dtype=jnp.int32) * col_count + my_col
    empty_block = jnp.zeros((tile_width, rhs_width), jnp.float32)

    def nothing_block():
        return empty_block

    def column_partial(rhs_local, target, lowest):

        def on_owner():
            column = lax.dynamic_index_in_dim(factor_tiles, target // col_count, 1, keepdims=False)
            weight = (row_index >= lowest).astype(jnp.float32)
            masked = rhs_local * weight[:, None, None]
            return jnp.einsum("aki,akr->ir", column, masked, precision=HIGHEST_PRECISION)

        return lax.cond(my_col == target % col_count, on_owner, nothing_block)

    def target_block(target):
        return lax.dynamic_index_in_dim(target_local, target // col_count, 0, keepdims=False)

    def advance(right_side, target, carried):
        rhs_local, factor_grad = carried
        local_slot = target // row_count
        holds_row = my_row == target % row_count
        is_owner = holds_row & (my_col == target % col_count)

        def solve_here():
            tile_row = lax.dynamic_index_in_dim(factor_tiles, local_slot, 0, keepdims=False)
            diagonal = lax.dynamic_index_in_dim(tile_row, target // col_count, 0, keepdims=False)
            return lax.linalg.triangular_solve(
                diagonal, right_side, left_side=True, lower=True, transpose_a=True
            )

        solved = lax.cond(is_owner, solve_here, nothing_block)
        arrived = broadcast(solved, "col", target % col_count)
        current = lax.dynamic_index_in_dim(rhs_local, local_slot, 0, keepdims=False)
        rhs_local = lax.dynamic_update_index_in_dim(
            rhs_local, jnp.where(holds_row, arrived, current), local_slot, 0
        )
        return (rhs_local, factor_grad)

    final_index = tile_count - 1
    carried = (
        jnp.zeros((local_rows, tile_width, rhs_width), jnp.float32),
        jnp.zeros((local_rows, local_cols, tile_width, tile_width), jnp.float32),
    )
    carried = advance(target_block(jnp.int32(final_index)), jnp.int32(final_index), carried)

    def sweep_step(offset, loop_state):
        carried, early_sum = loop_state
        target = final_index - 1 - offset
        rhs_local = carried[0]
        source = target + 1

        def compute_fresh():
            tile_row = lax.dynamic_index_in_dim(
                factor_tiles, source // row_count, 0, keepdims=False
            )
            tile_now = lax.dynamic_index_in_dim(tile_row, target // col_count, 0, keepdims=False)
            newest = lax.dynamic_index_in_dim(rhs_local, source // row_count, 0, keepdims=False)
            return jnp.dot(
                tile_now.T, newest, precision=HIGHEST_PRECISION, preferred_element_type=jnp.float32
            )

        fresh_owner = (my_row == source % row_count) & (my_col == target % col_count)
        fresh_term = lax.cond(fresh_owner, compute_fresh, nothing_block)
        moved_term = from_behind(fresh_term, "row", -1)
        following = jnp.maximum(target - 1, 0)
        next_partial = column_partial(rhs_local, following, source)
        next_sum = lax.psum(next_partial, "row")
        carried = advance(target_block(target) - early_sum - moved_term, target, carried)
        return (carried, next_sum)

    carried, unused_sum = lax.fori_loop(0, final_index, sweep_step, (carried, empty_block))
    rhs_local, factor_grad = carried
    products = -jnp.einsum("akr,blr->abkl", rhs_local, solution_local, precision=HIGHEST_PRECISION)
    masks = lower_mask(row_index[:, None, None, None], col_index[None, :, None, None], tile_width)
    factor_grad = jnp.where(masks, products, jnp.zeros_like(products))
    return (rhs_local[:, None], factor_grad[:, None, :, None])


def solution(mesh):
    placed = (
        P(None, "row", None, "col", None, None),
        P(None, "row", None, "col", None, None),
        P(None, "row", None, "col"),
        P(None, "col", None, None),
        P(None, "col", None, None),
    )
    return jax.shard_map(
        body,
        mesh=mesh,
        in_specs=placed,
        out_specs=(P(None, "row", None, None), P(None, "row", None, "col", None, None)),
        check_vma=False,
    )
```

profile of v0, /device:TPU:0, one launch (start us, length us, event | category | flops | bytes accessed | tf_op | source)
XLA Modules:
  0.0 2219.2 jit_solution(8826648313586827079)
XLA Ops:
  7.3 9.9 copy.12
  17.2 7.3 copy.11
  24.5 9.6 convert_select_fusion
  35.9 117.2 %all-reduce.5.cloned.1.call-done = f32[512,128]{1,0:T(8,128)} async-done(((f32[512,128]{1,0:T(8,128)}), f32[512,128]{1,0:T(8,128)}) %all-reduce.5.cloned.1.call-update) | async-done | bytes 262160 | tf_op jit(solution)/shard_map/psum | solution.py:11
  153.2 2048.1 %while.28 = (s32[]{:T(128)}, f32[4,512,128]{2,1,0:T(8,128)S(1)}, f32[512,128]{1,0:T(8,128)S(1)}, s32[]{:T(128)}, s32[]{:T(128)}, /*index=5*/f32[4,2,512,512]{2,3...) while((s32[]{:T(128)}, f32[4,512,128]{2,1,0:T(8,128)S(1)}, ...), condition=%wide.region_12.14_spmd.clone.clone, body=%wide.region_3.13_spmd.clone.clone.sunk | while | flops 2266480640 | bytes 54005560 | solution.py:116
  163.3 40.6 %all-reduce.9.cloned.1.call-done = f32[512,128]{1,0:T(8,128)} async-done(((f32[512,128]{1,0:T(8,128)}), f32[512,128]{1,0:T(8,128)}) %all-reduce.9.cloned.1.call-update) | async-done | bytes 262160 | tf_op jit(solution)/shard_map/while/body/eval_jaxpr/psum | solution.py:112
  204.9 86.8 %all-reduce.7.cloned.1.call-done = f32[512,128]{1,0:T(8,128)} async-done(((f32[512,128]{1,0:T(8,128)}), f32[512,128]{1,0:T(8,128)}) %all-reduce.7.cloned.1.call-update) | async-done | bytes 262160 | tf_op jit(solution)/shard_map/while/body/eval_jaxpr/psum | solution.py:11
  300.8 39.6 %all-reduce.9.cloned.1.call-done = f32[512,128]{1,0:T(8,128)} async-done(((f32[512,128]{1,0:T(8,128)}), f32[512,128]{1,0:T(8,128)}) %all-reduce.9.cloned.1.call-update) | async-done | bytes 262160 | tf_op jit(solution)/shard_map/while/body/eval_jaxpr/psum | solution.py:112
  341.4 85.4 %all-reduce.7.cloned.1.call-done = f32[512,128]{1,0:T(8,128)} async-done(((f32[512,128]{1,0:T(8,128)}), f32[512,128]{1,0:T(8,128)}) %all-reduce.7.cloned.1.call-update) | async-done | bytes 262160 | tf_op jit(solution)/shard_map/while/body/eval_jaxpr/psum | solution.py:11
  435.9 40.6 %all-reduce.9.cloned.1.call-done = f32[512,128]{1,0:T(8,128)} async-done(((f32[512,128]{1,0:T(8,128)}), f32[512,128]{1,0:T(8,128)}) %all-reduce.9.cloned.1.call-update) | async-done | bytes 262160 | tf_op jit(solution)/shard_map/while/body/eval_jaxpr/psum | solution.py:112
  477.4 85.9 %all-reduce.7.cloned.1.call-done = f32[512,128]{1,0:T(8,128)} async-done(((f32[512,128]{1,0:T(8,128)}), f32[512,128]{1,0:T(8,128)}) %all-reduce.7.cloned.1.call-update) | async-done | bytes 262160 | tf_op jit(solution)/shard_map/while/body/eval_jaxpr/psum | solution.py:11
  572.6 37.7 %all-reduce.9.cloned.1.call-done = f32[512,128]{1,0:T(8,128)} async-done(((f32[512,128]{1,0:T(8,128)}), f32[512,128]{1,0:T(8,128)}) %all-reduce.9.cloned.1.call-update) | async-done | bytes 262160 | tf_op jit(solution)/shard_map/while/body/eval_jaxpr/psum | solution.py:112
  611.3 88.0 %all-reduce.7.cloned.1.call-done = f32[512,128]{1,0:T(8,128)} async-done(((f32[512,128]{1,0:T(8,128)}), f32[512,128]{1,0:T(8,128)}) %all-reduce.7.cloned.1.call-update) | async-done | bytes 262160 | tf_op jit(solution)/shard_map/while/body/eval_jaxpr/psum | solution.py:11
  709.4 40.6 %all-reduce.9.cloned.1.call-done = f32[512,128]{1,0:T(8,128)} async-done(((f32[512,128]{1,0:T(8,128)}), f32[512,128]{1,0:T(8,128)}) %all-reduce.9.cloned.1.call-update) | async-done | bytes 262160 | tf_op jit(solution)/shard_map/while/body/eval_jaxpr/psum | solution.py:112
  751.0 86.8 %all-reduce.7.cloned.1.call-done = f32[512,128]{1,0:T(8,128)} async-done(((f32[512,128]{1,0:T(8,128)}), f32[512,128]{1,0:T(8,128)}) %all-reduce.7.cloned.1.call-update) | async-done | bytes 262160 | tf_op jit(solution)/shard_map/while/body/eval_jaxpr/psum | solution.py:11
  841.4 5.7 conditional.16
  841.4 5.7 fusion.11
  848.8 37.8 %all-reduce.9.cloned.1.call-done = f32[512,128]{1,0:T(8,128)} async-done(((f32[512,128]{1,0:T(8,128)}), f32[512,128]{1,0:T(8,128)}) %all-reduce.9.cloned.1.call-update) | async-done | bytes 262160 | tf_op jit(solution)/shard_map/while/body/eval_jaxpr/psum | solution.py:112
  887.5 85.3 %all-reduce.7.cloned.1.call-done = f32[512,128]{1,0:T(8,128)} async-done(((f32[512,128]{1,0:T(8,128)}), f32[512,128]{1,0:T(8,128)}) %all-reduce.7.cloned.1.call-update) | async-done | bytes 262160 | tf_op jit(solution)/shard_map/while/body/eval_jaxpr/psum | solution.py:11
  977.3 15.6 collective-permute-done
  992.9 65.2 %conditional.15 = (f32[512,128]{1,0:T(8,128)S(1)}) conditional(s32[]{:T(128)} %convert_element_type.68, () %tuple.144, (s32[]{:T(128)}, s32[]{:T(128)}, f32[4,2,512,512]{2,3,0,1:T(8,128)}, s32[]{:T(128)}, pred[]{:T(512)}, /*index=5*/pred[]{:T(512)}, s32[]{:T(128)}, f32[2,512,128]{2,1,0:T(8,128)}, f32[512,128]{1,0:T(8,128)S(1)}, ...), branch_computations={%region_6.7_spmd, %region_7.8_spmd} | conditional | flops 252690464 | bytes 22546512 | solution.py:76
  992.9 10.0 copy.8
  1004.2 10.6 while.27
  1014.8 40.1 %custom-call.5 = f32[4,128,128]{1,2,0:T(8,128)S(1)} custom-call(f32[4,128,128]{2,1,0:T(8,128)} %get-tuple-element.560), custom_call_target="InvertDiagBlocksLowerTriangular" | custom-call | tf_op jit(solution)/shard_map/while/body/eval_jaxpr/cond/branch_1_fun/triangular_solve/custom-call.1 | solution.py:72
  1059.8 48.9 %all-reduce.7.cloned.1.call-done = f32[512,128]{1,0:T(8,128)} async-done(((f32[512,128]{1,0:T(8,128)}), f32[512,128]{1,0:T(8,128)}) %all-reduce.7.cloned.1.call-update) | async-done | bytes 262160 | tf_op jit(solution)/shard_map/while/body/eval_jaxpr/psum | solution.py:11
  1118.0 37.9 %all-reduce.9.cloned.1.call-done = f32[512,128]{1,0:T(8,128)} async-done(((f32[512,128]{1,0:T(8,128)}), f32[512,128]{1,0:T(8,128)}) %all-reduce.9.cloned.1.call-update) | async-done | bytes 262160 | tf_op jit(solution)/shard_map/while/body/eval_jaxpr/psum | solution.py:112
  1156.9 88.0 %all-reduce.7.cloned.1.call-done = f32[512,128]{1,0:T(8,128)} async-done(((f32[512,128]{1,0:T(8,128)}), f32[512,128]{1,0:T(8,128)}) %all-reduce.7.cloned.1.call-update) | async-done | bytes 262160 | tf_op jit(solution)/shard_map/while/body/eval_jaxpr/psum | solution.py:11
  1255.0 40.6 %all-reduce.9.cloned.1.call-done = f32[512,128]{1,0:T(8,128)} async-done(((f32[512,128]{1,0:T(8,128)}), f32[512,128]{1,0:T(8,128)}) %all-reduce.9.cloned.1.call-update) | async-done | bytes 262160 | tf_op jit(solution)/shard_map/while/body/eval_jaxpr/psum | solution.py:112
  1296.5 86.8 %all-reduce.7.cloned.1.call-done = f32[512,128]{1,0:T(8,128)} async-done(((f32[512,128]{1,0:T(8,128)}), f32[512,128]{1,0:T(8,128)}) %all-reduce.7.cloned.1.call-update) | async-done | bytes 262160 | tf_op jit(solution)/shard_map/while/body/eval_jaxpr/psum | solution.py:11
  1392.5 39.6 %all-reduce.9.cloned.1.call-done = f32[512,128]{1,0:T(8,128)} async-done(((f32[512,128]{1,0:T(8,128)}), f32[512,128]{1,0:T(8,128)}) %all-reduce.9.cloned.1.call-update) | async-done | bytes 262160 | tf_op jit(solution)/shard_map/while/body/eval_jaxpr/psum | solution.py:112
  1433.0 85.3 %all-reduce.7.cloned.1.call-done = f32[512,128]{1,0:T(8,128)} async-done(((f32[512,128]{1,0:T(8,128)}), f32[512,128]{1,0:T(8,128)}) %all-reduce.7.cloned.1.call-update) | async-done | bytes 262160 | tf_op jit(solution)/shard_map/while/body/eval_jaxpr/psum | solution.py:11
  1527.5 40.6 %all-reduce.9.cloned.1.call-done = f32[512,128]{1,0:T(8,128)} async-done(((f32[512,128]{1,0:T(8,128)}), f32[512,128]{1,0:T(8,128)}) %all-reduce.9.cloned.1.call-update) | async-done | bytes 262160 | tf_op jit(solution)/shard_map/while/body/eval_jaxpr/psum | solution.py:112
  1569.1 85.9 %all-reduce.7.cloned.1.call-done = f32[512,128]{1,0:T(8,128)} async-done(((f32[512,128]{1,0:T(8,128)}), f32[512,128]{1,0:T(8,128)}) %all-reduce.7.cloned.1.call-update) | async-done | bytes 262160 | tf_op jit(solution)/shard_map/while/body/eval_jaxpr/psum | solution.py:11
  1664.2 37.7 %all-reduce.9.cloned.1.call-done = f32[512,128]{1,0:T(8,128)} async-done(((f32[512,128]{1,0:T(8,128)}), f32[512,128]{1,0:T(8,128)}) %all-reduce.9.cloned.1.call-update) | async-done | bytes 262160 | tf_op jit(solution)/shard_map/while/body/eval_jaxpr/psum | solution.py:112
  1702.9 88.1 %all-reduce.7.cloned.1.call-done = f32[512,128]{1,0:T(8,128)} async-done(((f32[512,128]{1,0:T(8,128)}), f32[512,128]{1,0:T(8,128)}) %all-reduce.7.cloned.1.call-update) | async-done | bytes 262160 | tf_op jit(solution)/shard_map/while/body/eval_jaxpr/psum | solution.py:11
  1801.1 40.6 %all-reduce.9.cloned.1.call-done = f32[512,128]{1,0:T(8,128)} async-done(((f32[512,128]{1,0:T(8,128)}), f32[512,128]{1,0:T(8,128)}) %all-reduce.9.cloned.1.call-update) | async-done | bytes 262160 | tf_op jit(solution)/shard_map/while/body/eval_jaxpr/psum | solution.py:112
  1842.6 86.8 %all-reduce.7.cloned.1.call-done = f32[512,128]{1,0:T(8,128)} async-done(((f32[512,128]{1,0:T(8,128)}), f32[512,128]{1,0:T(8,128)}) %all-reduce.7.cloned.1.call-update) | async-done | bytes 262160 | tf_op jit(solution)/shard_map/while/body/eval_jaxpr/psum | solution.py:11
  1933.0 5.7 conditional.16
  1940.4 37.8 %all-reduce.9.cloned.1.call-done = f32[512,128]{1,0:T(8,128)} async-done(((f32[512,128]{1,0:T(8,128)}), f32[512,128]{1,0:T(8,128)}) %all-reduce.9.cloned.1.call-update) | async-done | bytes 262160 | tf_op jit(solution)/shard_map/while/body/eval_jaxpr/psum | solution.py:112
  1979.1 85.3 %all-reduce.7.cloned.1.call-done = f32[512,128]{1,0:T(8,128)} async-done(((f32[512,128]{1,0:T(8,128)}), f32[512,128]{1,0:T(8,128)}) %all-reduce.7.cloned.1.call-update) | async-done | bytes 262160 | tf_op jit(solution)/shard_map/while/body/eval_jaxpr/psum | solution.py:11
  2068.1 5.7 conditional.16
  2074.6 9.9 collective-permute-done
  2084.6 65.1 %conditional.15 = (f32[512,128]{1,0:T(8,128)S(1)}) conditional(s32[]{:T(128)} %convert_element_type.68, () %tuple.144, (s32[]{:T(128)}, s32[]{:T(128)}, f32[4,2,512,512]{2,3,0,1:T(8,128)}, s32[]{:T(128)}, pred[]{:T(512)}, /*index=5*/pred[]{:T(512)}, s32[]{:T(128)}, f32[2,512,128]{2,1,0:T(8,128)}, f32[512,128]{1,0:T(8,128)S(1)}, ...), branch_computations={%region_6.7_spmd, %region_7.8_spmd} | conditional | flops 252690464 | bytes 22546512 | solution.py:76
  2084.6 10.0 copy.8
  2095.9 10.6 while.27
  2106.5 40.1 %custom-call.5 = f32[4,128,128]{1,2,0:T(8,128)S(1)} custom-call(f32[4,128,128]{2,1,0:T(8,128)} %get-tuple-element.560), custom_call_target="InvertDiagBlocksLowerTriangular" | custom-call | tf_op jit(solution)/shard_map/while/body/eval_jaxpr/cond/branch_1_fun/triangular_solve/custom-call.1 | solution.py:72
  2151.5 48.9 %all-reduce.7.cloned.1.call-done = f32[512,128]{1,0:T(8,128)} async-done(((f32[512,128]{1,0:T(8,128)}), f32[512,128]{1,0:T(8,128)}) %all-reduce.7.cloned.1.call-update) | async-done | bytes 262160 | tf_op jit(solution)/shard_map/while/body/eval_jaxpr/psum | solution.py:11
  2201.4 11.0 fusion.55
  (350 shorter events, 182.1 us)
Async XLA Ops:
  7.2 2194.2 %copy-start = (f32[2,1,512,128]{3,2,1,0:T(8,128)S(1)}, f32[2,1,512,128]{3,2,1,0:T(8,128)}, u32[]{:S(2)}) copy-start(f32[2,1,512,128]{3,2,1,0:T(8,128)} %param.20) | copy-start | bytes 1572868
  7.2 145.9 %all-reduce.5.cloned.1.call-start = ((), (), s32[]{:S(2)}) async-start(), calls=%async_computation | async-start | bytes 524288 | tf_op jit(solution)/shard_map/psum | solution.py:11
  7.2 17.2 copy-start.3
  153.3 50.7 %all-reduce.9.cloned.1.call-start = ((), (), s32[]{:S(2)}) async-start(), calls=%async_computation.2 | async-start | bytes 524288 | tf_op jit(solution)/shard_map/while/body/eval_jaxpr/psum | solution.py:112
  153.4 9.1 collective-permute-start
  158.5 133.2 %all-reduce.7.cloned.1.call-start = ((), (), s32[]{:S(2)}) async-start(), calls=%async_computation.1 | async-start | bytes 524288 | tf_op jit(solution)/shard_map/while/body/eval_jaxpr/psum | solution.py:11
  291.7 48.7 %all-reduce.9.cloned.1.call-start = ((), (), s32[]{:S(2)}) async-start(), calls=%async_computation.2 | async-start | bytes 524288 | tf_op jit(solution)/shard_map/while/body/eval_jaxpr/psum | solution.py:112
  291.9 8.1 collective-permute-start
  296.0 130.7 %all-reduce.7.cloned.1.call-start = ((), (), s32[]{:S(2)}) async-start(), calls=%async_computation.1 | async-start | bytes 524288 | tf_op jit(solution)/shard_map/while/body/eval_jaxpr/psum | solution.py:11
  426.8 49.7 %all-reduce.9.cloned.1.call-start = ((), (), s32[]{:S(2)}) async-start(), calls=%async_computation.2 | async-start | bytes 524288 | tf_op jit(solution)/shard_map/while/body/eval_jaxpr/psum | solution.py:112
  426.9 8.1 collective-permute-start
  431.1 132.2 %all-reduce.7.cloned.1.call-start = ((), (), s32[]{:S(2)}) async-start(), calls=%async_computation.1 | async-start | bytes 524288 | tf_op jit(solution)/shard_map/while/body/eval_jaxpr/psum | solution.py:11
  564.3 46.0 %all-reduce.9.cloned.1.call-start = ((), (), s32[]{:S(2)}) async-start(), calls=%async_computation.2 | async-start | bytes 524288 | tf_op jit(solution)/shard_map/while/body/eval_jaxpr/psum | solution.py:112
  564.5 7.3 collective-permute-start
  567.7 131.6 %all-reduce.7.cloned.1.call-start = ((), (), s32[]{:S(2)}) async-start(), calls=%async_computation.1 | async-start | bytes 524288 | tf_op jit(solution)/shard_map/while/body/eval_jaxpr/psum | solution.py:11
  699.4 50.6 %all-reduce.9.cloned.1.call-start = ((), (), s32[]{:S(2)}) async-start(), calls=%async_computation.2 | async-start | bytes 524288 | tf_op jit(solution)/shard_map/while/body/eval_jaxpr/psum | solution.py:112
  699.5 9.1 collective-permute-start
  704.6 133.1 %all-reduce.7.cloned.1.call-start = ((), (), s32[]{:S(2)}) async-start(), calls=%async_computation.1 | async-start | bytes 524288 | tf_op jit(solution)/shard_map/while/body/eval_jaxpr/psum | solution.py:11
  837.8 48.7 %all-reduce.9.cloned.1.call-start = ((), (), s32[]{:S(2)}) async-start(), calls=%async_computation.2 | async-start | bytes 524288 | tf_op jit(solution)/shard_map/while/body/eval_jaxpr/psum | solution.py:112
  838.0 10.0 collective-permute-start
  847.8 125.0 %all-reduce.7.cloned.1.call-start = ((), (), s32[]{:S(2)}) async-start(), calls=%async_computation.1 | async-start | bytes 524288 | tf_op jit(solution)/shard_map/while/body/eval_jaxpr/psum | solution.py:11
  972.9 86.0 %all-reduce.9.cloned.1.call-start = ((), (), s32[]{:S(2)}) async-start(), calls=%async_computation.2 | async-start | bytes 524288 | tf_op jit(solution)/shard_map/while/body/eval_jaxpr/psum | solution.py:112
  973.0 19.9 collective-permute-start
  977.2 131.5 %all-reduce.7.cloned.1.call-start = ((), (), s32[]{:S(2)}) async-start(), calls=%async_computation.1 | async-start | bytes 524288 | tf_op jit(solution)/shard_map/while/body/eval_jaxpr/psum | solution.py:11
  1109.7 46.2 %all-reduce.9.cloned.1.call-start = ((), (), s32[]{:S(2)}) async-start(), calls=%async_computation.2 | async-start | bytes 524288 | tf_op jit(solution)/shard_map/while/body/eval_jaxpr/psum | solution.py:112
  1109.9 7.3 collective-permute-start
  1113.1 131.8 %all-reduce.7.cloned.1.call-start = ((), (), s32[]{:S(2)}) async-start(), calls=%async_computation.1 | async-start | bytes 524288 | tf_op jit(solution)/shard_map/while/body/eval_jaxpr/psum | solution.py:11
  1244.9 50.7 %all-reduce.9.cloned.1.call-start = ((), (), s32[]{:S(2)}) async-start(), calls=%async_computation.2 | async-start | bytes 524288 | tf_op jit(solution)/shard_map/while/body/eval_jaxpr/psum | solution.py:112
  1245.1 9.1 collective-permute-start
  1250.2 133.2 %all-reduce.7.cloned.1.call-start = ((), (), s32[]{:S(2)}) async-start(), calls=%async_computation.1 | async-start | bytes 524288 | tf_op jit(solution)/shard_map/while/body/eval_jaxpr/psum | solution.py:11
  1383.4 48.7 %all-reduce.9.cloned.1.call-start = ((), (), s32[]{:S(2)}) async-start(), calls=%async_computation.2 | async-start | bytes 524288 | tf_op jit(solution)/shard_map/while/body/eval_jaxpr/psum | solution.py:112
  1383.5 8.1 collective-permute-start
  1387.7 130.7 %all-reduce.7.cloned.1.call-start = ((), (), s32[]{:S(2)}) async-start(), calls=%async_computation.1 | async-start | bytes 524288 | tf_op jit(solution)/shard_map/while/body/eval_jaxpr/psum | solution.py:11
  1518.4 49.7 %all-reduce.9.cloned.1.call-start = ((), (), s32[]{:S(2)}) async-start(), calls=%async_computation.2 | async-start | bytes 524288 | tf_op jit(solution)/shard_map/while/body/eval_jaxpr/psum | solution.py:112
  1518.6 8.1 collective-permute-start
  1522.7 132.2 %all-reduce.7.cloned.1.call-start = ((), (), s32[]{:S(2)}) async-start(), calls=%async_computation.1 | async-start | bytes 524288 | tf_op jit(solution)/shard_map/while/body/eval_jaxpr/psum | solution.py:11
  1656.0 46.0 %all-reduce.9.cloned.1.call-start = ((), (), s32[]{:S(2)}) async-start(), calls=%async_computation.2 | async-start | bytes 524288 | tf_op jit(solution)/shard_map/while/body/eval_jaxpr/psum | solution.py:112
  1656.1 7.3 collective-permute-start
  1659.3 131.6 %all-reduce.7.cloned.1.call-start = ((), (), s32[]{:S(2)}) async-start(), calls=%async_computation.1 | async-start | bytes 524288 | tf_op jit(solution)/shard_map/while/body/eval_jaxpr/psum | solution.py:11
  1791.0 50.6 %all-reduce.9.cloned.1.call-start = ((), (), s32[]{:S(2)}) async-start(), calls=%async_computation.2 | async-start | bytes 524288 | tf_op jit(solution)/shard_map/while/body/eval_jaxpr/psum | solution.py:112
  1791.2 9.1 collective-permute-start
  1796.3 133.1 %all-reduce.7.cloned.1.call-start = ((), (), s32[]{:S(2)}) async-start(), calls=%async_computation.1 | async-start | bytes 524288 | tf_op jit(solution)/shard_map/while/body/eval_jaxpr/psum | solution.py:11
  1929.5 48.7 %all-reduce.9.cloned.1.call-start = ((), (), s32[]{:S(2)}) async-start(), calls=%async_computation.2 | async-start | bytes 524288 | tf_op jit(solution)/shard_map/while/body/eval_jaxpr/psum | solution.py:112
  1929.6 9.9 collective-permute-start
  1939.4 125.0 %all-reduce.7.cloned.1.call-start = ((), (), s32[]{:S(2)}) async-start(), calls=%async_computation.1 | async-start | bytes 524288 | tf_op jit(solution)/shard_map/while/body/eval_jaxpr/psum | solution.py:11
  2064.5 86.0 %all-reduce.9.cloned.1.call-start = ((), (), s32[]{:S(2)}) async-start(), calls=%async_computation.2 | async-start | bytes 524288 | tf_op jit(solution)/shard_map/while/body/eval_jaxpr/psum | solution.py:112
  2064.7 19.9 collective-permute-start
  2074.5 125.8 %all-reduce.7.cloned.1.call-start = ((), (), s32[]{:S(2)}) async-start(), calls=%async_computation.1 | async-start | bytes 524288 | tf_op jit(solution)/shard_map/while/body/eval_jaxpr/psum | solution.py:11
  (16 other events, 22.0 us)
Sparse Core Ops, SparseCore 0:
  35.2 117.8 all-reduce.4
  158.6 45.2 all-reduce.8
  207.6 84.0 all-reduce.6
  296.2 44.2 all-reduce.8
  343.9 82.7 all-reduce.6
  431.2 45.2 all-reduce.8
  480.1 83.1 all-reduce.6
  567.8 42.4 all-reduce.8
  614.0 85.3 all-reduce.6
  704.8 45.2 all-reduce.8
  753.7 84.0 all-reduce.6
  847.9 38.5 all-reduce.8
  890.2 82.6 all-reduce.6
  977.3 44.9 all-reduce.8
  1058.9 49.7 all-reduce.6
  1113.2 42.6 all-reduce.8
  1159.4 85.4 all-reduce.6
  1250.3 45.2 all-reduce.8
  1299.2 84.0 all-reduce.6
  1387.8 44.2 all-reduce.8
  1435.7 82.6 all-reduce.6
  1522.8 45.2 all-reduce.8
  1571.7 83.1 all-reduce.6
  1659.5 42.4 all-reduce.8
  1705.6 85.3 all-reduce.6
  1796.4 45.2 all-reduce.8
  1845.1 84.2 all-reduce.6
  1939.6 38.5 all-reduce.8
  1981.8 82.6 all-reduce.6
  2074.7 45.0 all-reduce.8
  2150.6 49.7 all-reduce.6
where the time goes:
time: 2220 us
  waiting for transfers between devices  1920 us (86%)
  other arithmetic  111 us (5%)
  local copies, waits for them, and re-layouts  84.6 us (4%)
  starting transfers between devices  53 us (2%)
  matrix products  32.1 us (1%)
    psum x16, waiting for transfers between devices, broadcast(): return lax.psum(jnp.where(mine, value, jnp.zeros_like(value)), axis)  1340 us
    psum x15, waiting for transfers between devices, sweep_step(): next_sum = lax.psum(next_partial, 'row')  512 us
    another operation x10, other arithmetic, solve_here(): lax.linalg.triangular_solve(diagonal, right_side, left_side=True, lower=T...  83 us
    ppermute x15, waiting for transfers between devices, from_behind(): lax.ppermute(value, axis, [(i, (i + by) % size) for i in range(size)])  68.5 us
    ppermute x15, starting transfers between devices, from_behind(): lax.ppermute(value, axis, [(i, (i + by) % size) for i in range(size)])  51.7 us
  transfers between devices with their start and end apart: 46, of which 42 were waited for; matrix products, arithmetic and copies ran while one was open for 8% of the time, Pallas kernels for 0%

commit v1 on v0

--- a/solution.py
+++ b/solution.py
@@ -8,7 +8,12 @@
 
 def broadcast(value, axis, root):
     mine = lax.axis_index(axis) == root
-    return lax.psum(jnp.where(mine, value, jnp.zeros_like(value)), axis)
+
+    def frame_refer(a0):
+        block_last = lax.all_gather(a0, axis_name=axis)
+        return jnp.sum(block_last, axis=0)
+
+    return frame_refer(jnp.where(mine, value, jnp.zeros_like(value)))
 
 
 def from_behind(value, axis, by):

time: 2220 us -> 1830 us (0.82)
  waiting for transfers between devices: 1920 us -> 1510 us
  other arithmetic: 111 us -> 135 us
    psum x16 -> x0, waiting for transfers between devices: 1340 us -> none  [broadcast(): return lax.psum(jnp.where(mine, value, jnp.zeros_like(value)), axis)]
    all_gather x0 -> x16, waiting for transfers between devices: none -> 919 us  [frame_refer(): block_last = lax.all_gather(a0, axis_name=axis)]
    reduce_sum x0 -> x16, other arithmetic: none -> 27.5 us  [frame_refer(): return jnp.sum(block_last, axis=0)]
  transfers between devices with their start and end apart: 46 -> 46, of which waited for: 42 -> 42; matrix products, arithmetic and copies ran while one was open for 8% -> 9% of each run, Pallas kernels for 0% -> 0%
where the time goes in v1:
time: 1830 us
  waiting for transfers between devices  1510 us (83%)
  other arithmetic  135 us (7%)
  local copies, waits for them, and re-layouts  84.2 us (5%)
  starting transfers between devices  52 us (3%)
  matrix products  32.1 us (2%)
    all_gather x16, waiting for transfers between devices, frame_refer(): block_last = lax.all_gather(a0, axis_name=axis)  919 us
    psum x15, waiting for transfers between devices, sweep_step(): next_sum = lax.psum(next_partial, 'row')  507 us
    another operation x10, other arithmetic, solve_here(): lax.linalg.triangular_solve(diagonal, right_side, left_side=True, lower=T...  83 us
    ppermute x15, waiting for transfers between devices, from_behind(): lax.ppermute(value, axis, [(i, (i + by) % size) for i in range(size)])  79.5 us
    ppermute x15, starting transfers between devices, from_behind(): lax.ppermute(value, axis, [(i, (i + by) % size) for i in range(size)])  50.7 us
  transfers between devices with their start and end apart: 46, of which 42 were waited for; matrix products, arithmetic and copies ran while one was open for 9% of the time, Pallas kernels for 0%

profile of v1, /device:TPU:0, one launch (start us, length us, event | category | flops | bytes accessed | tf_op | source)
XLA Modules:
  0.0 1828.8 jit_solution(14196743532766641498)
XLA Ops:
  8.1 9.9 copy.12
  18.0 7.3 copy.11
  25.3 9.6 convert_select_fusion
  36.8 91.1 %all-gather.9.cloned.1.call-done = f32[4096,128]{1,0:T(8,128)} async-done(((f32[512,128]{1,0:T(8,128)}), f32[4096,128]{1,0:T(8,128)}) %all-gather.9.cloned.1.call-update) | async-done | bytes 2097168 | tf_op jit(solution)/shard_map/all_gather | solution.py:13
  129.7 1680.7 %while.28 = (s32[]{:T(128)}, f32[4,512,128]{2,1,0:T(8,128)S(1)}, f32[512,128]{1,0:T(8,128)S(1)}, s32[]{:T(128)}, s32[]{:T(128)}, /*index=5*/f32[4,2,512,512]{2,3...) while((s32[]{:T(128)}, f32[4,512,128]{2,1,0:T(8,128)S(1)}, ...), condition=%wide.region_12.14_spmd.clone.clone, body=%wide.region_3.13_spmd.clone.clone.sunk | while | flops 2266873856 | bytes 61345600 | solution.py:121
  140.0 40.0 %all-reduce.3.cloned.1.call-done = f32[512,128]{1,0:T(8,128)} async-done(((f32[512,128]{1,0:T(8,128)}), f32[512,128]{1,0:T(8,128)}) %all-reduce.3.cloned.1.call-update) | async-done | bytes 262160 | tf_op jit(solution)/shard_map/while/body/eval_jaxpr/psum | solution.py:117
  181.0 60.5 %all-gather.11.cloned.1.call-done = f32[4096,128]{1,0:T(8,128)} async-done(((f32[512,128]{1,0:T(8,128)}), f32[4096,128]{1,0:T(8,128)}) %all-gather.11.cloned.1.call-update) | async-done | bytes 2097168 | tf_op jit(solution)/shard_map/while/body/eval_jaxpr/all_gather | solution.py:13
  253.6 39.5 %all-reduce.3.cloned.1.call-done = f32[512,128]{1,0:T(8,128)} async-done(((f32[512,128]{1,0:T(8,128)}), f32[512,128]{1,0:T(8,128)}) %all-reduce.3.cloned.1.call-update) | async-done | bytes 262160 | tf_op jit(solution)/shard_map/while/body/eval_jaxpr/psum | solution.py:117
  294.1 59.0 %all-gather.11.cloned.1.call-done = f32[4096,128]{1,0:T(8,128)} async-done(((f32[512,128]{1,0:T(8,128)}), f32[4096,128]{1,0:T(8,128)}) %all-gather.11.cloned.1.call-update) | async-done | bytes 2097168 | tf_op jit(solution)/shard_map/while/body/eval_jaxpr/all_gather | solution.py:13
  365.1 39.0 %all-reduce.3.cloned.1.call-done = f32[512,128]{1,0:T(8,128)} async-done(((f32[512,128]{1,0:T(8,128)}), f32[512,128]{1,0:T(8,128)}) %all-reduce.3.cloned.1.call-update) | async-done | bytes 262160 | tf_op jit(solution)/shard_map/while/body/eval_jaxpr/psum | solution.py:117
  405.1 59.7 %all-gather.11.cloned.1.call-done = f32[4096,128]{1,0:T(8,128)} async-done(((f32[512,128]{1,0:T(8,128)}), f32[4096,128]{1,0:T(8,128)}) %all-gather.11.cloned.1.call-update) | async-done | bytes 2097168 | tf_op jit(solution)/shard_map/while/body/eval_jaxpr/all_gather | solution.py:13
  476.8 37.8 %all-reduce.3.cloned.1.call-done = f32[512,128]{1,0:T(8,128)} async-done(((f32[512,128]{1,0:T(8,128)}), f32[512,128]{1,0:T(8,128)}) %all-reduce.3.cloned.1.call-update) | async-done | bytes 262160 | tf_op jit(solution)/shard_map/while/body/eval_jaxpr/psum | solution.py:117
  515.5 61.7 %all-gather.11.cloned.1.call-done = f32[4096,128]{1,0:T(8,128)} async-done(((f32[512,128]{1,0:T(8,128)}), f32[4096,128]{1,0:T(8,128)}) %all-gather.11.cloned.1.call-update) | async-done | bytes 2097168 | tf_op jit(solution)/shard_map/while/body/eval_jaxpr/all_gather | solution.py:13
  589.4 40.0 %all-reduce.3.cloned.1.call-done = f32[512,128]{1,0:T(8,128)} async-done(((f32[512,128]{1,0:T(8,128)}), f32[512,128]{1,0:T(8,128)}) %all-reduce.3.cloned.1.call-update) | async-done | bytes 262160 | tf_op jit(solution)/shard_map/while/body/eval_jaxpr/psum | solution.py:117
  630.4 60.5 %all-gather.11.cloned.1.call-done = f32[4096,128]{1,0:T(8,128)} async-done(((f32[512,128]{1,0:T(8,128)}), f32[4096,128]{1,0:T(8,128)}) %all-gather.11.cloned.1.call-update) | async-done | bytes 2097168 | tf_op jit(solution)/shard_map/while/body/eval_jaxpr/all_gather | solution.py:13
  696.2 5.7 conditional.16
  696.2 5.7 fusion.11
  703.6 38.1 %all-reduce.3.cloned.1.call-done = f32[512,128]{1,0:T(8,128)} async-done(((f32[512,128]{1,0:T(8,128)}), f32[512,128]{1,0:T(8,128)}) %all-reduce.3.cloned.1.call-update) | async-done | bytes 262160 | tf_op jit(solution)/shard_map/while/body/eval_jaxpr/psum | solution.py:117
  742.6 59.0 %all-gather.11.cloned.1.call-done = f32[4096,128]{1,0:T(8,128)} async-done(((f32[512,128]{1,0:T(8,128)}), f32[4096,128]{1,0:T(8,128)}) %all-gather.11.cloned.1.call-update) | async-done | bytes 2097168 | tf_op jit(solution)/shard_map/while/body/eval_jaxpr/all_gather | solution.py:13
  807.9 14.6 collective-permute-done
  822.5 65.2 %conditional.15 = (f32[512,128]{1,0:T(8,128)S(1)}) conditional(s32[]{:T(128)} %convert_element_type.68, () %tuple.144, (s32[]{:T(128)}, s32[]{:T(128)}, f32[4,2,512,512]{2,3,0,1:T(8,128)}, s32[]{:T(128)}, pred[]{:T(512)}, /*index=5*/pred[]{:T(512)}, s32[]{:T(128)}, f32[2,512,128]{2,1,0:T(8,128)}, f32[512,128]{1,0:T(8,128)S(1)}, ...), branch_computations={%region_6.7_spmd, %region_7.8_spmd} | conditional | flops 252690464 | bytes 22546512 | solution.py:81
  822.5 10.0 copy.8
  833.8 10.6 while.27
  844.4 40.1 %custom-call.5 = f32[4,128,128]{1,2,0:T(8,128)S(1)} custom-call(f32[4,128,128]{2,1,0:T(8,128)} %get-tuple-element.560), custom_call_target="InvertDiagBlocksLowerTriangular" | custom-call | tf_op jit(solution)/shard_map/while/body/eval_jaxpr/cond/branch_1_fun/triangular_solve/custom-call.1 | solution.py:77
  889.4 22.6 %all-gather.11.cloned.1.call-done = f32[4096,128]{1,0:T(8,128)} async-done(((f32[512,128]{1,0:T(8,128)}), f32[4096,128]{1,0:T(8,128)}) %all-gather.11.cloned.1.call-update) | async-done | bytes 2097168 | tf_op jit(solution)/shard_map/while/body/eval_jaxpr/all_gather | solution.py:13
  924.1 37.7 %all-reduce.3.cloned.1.call-done = f32[512,128]{1,0:T(8,128)} async-done(((f32[512,128]{1,0:T(8,128)}), f32[512,128]{1,0:T(8,128)}) %all-reduce.3.cloned.1.call-update) | async-done | bytes 262160 | tf_op jit(solution)/shard_map/while/body/eval_jaxpr/psum | solution.py:117
  962.8 61.7 %all-gather.11.cloned.1.call-done = f32[4096,128]{1,0:T(8,128)} async-done(((f32[512,128]{1,0:T(8,128)}), f32[4096,128]{1,0:T(8,128)}) %all-gather.11.cloned.1.call-update) | async-done | bytes 2097168 | tf_op jit(solution)/shard_map/while/body/eval_jaxpr/all_gather | solution.py:13
  1036.6 40.0 %all-reduce.3.cloned.1.call-done = f32[512,128]{1,0:T(8,128)} async-done(((f32[512,128]{1,0:T(8,128)}), f32[512,128]{1,0:T(8,128)}) %all-reduce.3.cloned.1.call-update) | async-done | bytes 262160 | tf_op jit(solution)/shard_map/while/body/eval_jaxpr/psum | solution.py:117
  1077.5 60.5 %all-gather.11.cloned.1.call-done = f32[4096,128]{1,0:T(8,128)} async-done(((f32[512,128]{1,0:T(8,128)}), f32[4096,128]{1,0:T(8,128)}) %all-gather.11.cloned.1.call-update) | async-done | bytes 2097168 | tf_op jit(solution)/shard_map/while/body/eval_jaxpr/all_gather | solution.py:13
  1150.2 39.5 %all-reduce.3.cloned.1.call-done = f32[512,128]{1,0:T(8,128)} async-done(((f32[512,128]{1,0:T(8,128)}), f32[512,128]{1,0:T(8,128)}) %all-reduce.3.cloned.1.call-update) | async-done | bytes 262160 | tf_op jit(solution)/shard_map/while/body/eval_jaxpr/psum | solution.py:117
  1190.7 59.0 %all-gather.11.cloned.1.call-done = f32[4096,128]{1,0:T(8,128)} async-done(((f32[512,128]{1,0:T(8,128)}), f32[4096,128]{1,0:T(8,128)}) %all-gather.11.cloned.1.call-update) | async-done | bytes 2097168 | tf_op jit(solution)/shard_map/while/body/eval_jaxpr/all_gather | solution.py:13
  1261.7 39.0 %all-reduce.3.cloned.1.call-done = f32[512,128]{1,0:T(8,128)} async-done(((f32[512,128]{1,0:T(8,128)}), f32[512,128]{1,0:T(8,128)}) %all-reduce.3.cloned.1.call-update) | async-done | bytes 262160 | tf_op jit(solution)/shard_map/while/body/eval_jaxpr/psum | solution.py:117
  1301.7 59.7 %all-gather.11.cloned.1.call-done = f32[4096,128]{1,0:T(8,128)} async-done(((f32[512,128]{1,0:T(8,128)}), f32[4096,128]{1,0:T(8,128)}) %all-gather.11.cloned.1.call-update) | async-done | bytes 2097168 | tf_op jit(solution)/shard_map/while/body/eval_jaxpr/all_gather | solution.py:13
  1373.4 37.8 %all-reduce.3.cloned.1.call-done = f32[512,128]{1,0:T(8,128)} async-done(((f32[512,128]{1,0:T(8,128)}), f32[512,128]{1,0:T(8,128)}) %all-reduce.3.cloned.1.call-update) | async-done | bytes 262160 | tf_op jit(solution)/shard_map/while/body/eval_jaxpr/psum | solution.py:117
  1412.1 61.7 %all-gather.11.cloned.1.call-done = f32[4096,128]{1,0:T(8,128)} async-done(((f32[512,128]{1,0:T(8,128)}), f32[4096,128]{1,0:T(8,128)}) %all-gather.11.cloned.1.call-update) | async-done | bytes 2097168 | tf_op jit(solution)/shard_map/while/body/eval_jaxpr/all_gather | solution.py:13
  1486.0 40.0 %all-reduce.3.cloned.1.call-done = f32[512,128]{1,0:T(8,128)} async-done(((f32[512,128]{1,0:T(8,128)}), f32[512,128]{1,0:T(8,128)}) %all-reduce.3.cloned.1.call-update) | async-done | bytes 262160 | tf_op jit(solution)/shard_map/while/body/eval_jaxpr/psum | solution.py:117
  1527.0 60.5 %all-gather.11.cloned.1.call-done = f32[4096,128]{1,0:T(8,128)} async-done(((f32[512,128]{1,0:T(8,128)}), f32[4096,128]{1,0:T(8,128)}) %all-gather.11.cloned.1.call-update) | async-done | bytes 2097168 | tf_op jit(solution)/shard_map/while/body/eval_jaxpr/all_gather | solution.py:13
  1592.8 5.7 conditional.16
  1600.2 38.1 %all-reduce.3.cloned.1.call-done = f32[512,128]{1,0:T(8,128)} async-done(((f32[512,128]{1,0:T(8,128)}), f32[512,128]{1,0:T(8,128)}) %all-reduce.3.cloned.1.call-update) | async-done | bytes 262160 | tf_op jit(solution)/shard_map/while/body/eval_jaxpr/psum | solution.py:117
  1639.2 59.0 %all-gather.11.cloned.1.call-done = f32[4096,128]{1,0:T(8,128)} async-done(((f32[512,128]{1,0:T(8,128)}), f32[4096,128]{1,0:T(8,128)}) %all-gather.11.cloned.1.call-update) | async-done | bytes 2097168 | tf_op jit(solution)/shard_map/while/body/eval_jaxpr/all_gather | solution.py:13
  1703.6 5.7 conditional.16
  1710.1 9.0 collective-permute-done
  1719.1 65.1 %conditional.15 = (f32[512,128]{1,0:T(8,128)S(1)}) conditional(s32[]{:T(128)} %convert_element_type.68, () %tuple.144, (s32[]{:T(128)}, s32[]{:T(128)}, f32[4,2,512,512]{2,3,0,1:T(8,128)}, s32[]{:T(128)}, pred[]{:T(512)}, /*index=5*/pred[]{:T(512)}, s32[]{:T(128)}, f32[2,512,128]{2,1,0:T(8,128)}, f32[512,128]{1,0:T(8,128)S(1)}, ...), branch_computations={%region_6.7_spmd, %region_7.8_spmd} | conditional | flops 252690464 | bytes 22546512 | solution.py:81
  1719.1 10.0 copy.8
  1730.4 10.6 while.27
  1741.0 40.1 %custom-call.5 = f32[4,128,128]{1,2,0:T(8,128)S(1)} custom-call(f32[4,128,128]{2,1,0:T(8,128)} %get-tuple-element.560), custom_call_target="InvertDiagBlocksLowerTriangular" | custom-call | tf_op jit(solution)/shard_map/while/body/eval_jaxpr/cond/branch_1_fun/triangular_solve/custom-call.1 | solution.py:77
  1786.0 22.6 %all-gather.11.cloned.1.call-done = f32[4096,128]{1,0:T(8,128)} async-done(((f32[512,128]{1,0:T(8,128)}), f32[4096,128]{1,0:T(8,128)}) %all-gather.11.cloned.1.call-update) | async-done | bytes 2097168 | tf_op jit(solution)/shard_map/while/body/eval_jaxpr/all_gather | solution.py:13
  1810.4 11.0 fusion.56
  (351 shorter events, 217.7 us)
Async XLA Ops:
  8.0 1802.4 %copy-start = (f32[2,1,512,128]{3,2,1,0:T(8,128)S(1)}, f32[2,1,512,128]{3,2,1,0:T(8,128)}, u32[]{:S(2)}) copy-start(f32[2,1,512,128]{3,2,1,0:T(8,128)} %param.20) | copy-start | bytes 1572868
  8.0 119.8 %all-gather.9.cloned.1.call-start = ((), (), s32[]{:S(2)}) async-start(), calls=%async_computation | async-start | bytes 2359296 | tf_op jit(solution)/shard_map/all_gather | solution.py:13
  8.1 17.2 copy-start.3
  129.7 50.3 %all-reduce.3.cloned.1.call-start = ((), (), s32[]{:S(2)}) async-start(), calls=%async_computation.2 | async-start | bytes 524288 | tf_op jit(solution)/shard_map/while/body/eval_jaxpr/psum | solution.py:117
  129.8 9.3 collective-permute-start
  134.0 107.5 %all-gather.11.cloned.1.call-start = ((), (), s32[]{:S(2)}) async-start(), calls=%async_computation.1 | async-start | bytes 2359296 | tf_op jit(solution)/shard_map/while/body/eval_jaxpr/all_gather | solution.py:13
  243.3 49.8 %all-reduce.3.cloned.1.call-start = ((), (), s32[]{:S(2)}) async-start(), calls=%async_computation.2 | async-start | bytes 524288 | tf_op jit(solution)/shard_map/while/body/eval_jaxpr/psum | solution.py:117
  243.4 9.3 collective-permute-start
  247.6 105.5 %all-gather.11.cloned.1.call-start = ((), (), s32[]{:S(2)}) async-start(), calls=%async_computation.1 | async-start | bytes 2359296 | tf_op jit(solution)/shard_map/while/body/eval_jaxpr/all_gather | solution.py:13
  354.9 49.3 %all-reduce.3.cloned.1.call-start = ((), (), s32[]{:S(2)}) async-start(), calls=%async_computation.2 | async-start | bytes 524288 | tf_op jit(solution)/shard_map/while/body/eval_jaxpr/psum | solution.py:117
  355.0 9.3 collective-permute-start
  359.2 105.6 %all-gather.11.cloned.1.call-start = ((), (), s32[]{:S(2)}) async-start(), calls=%async_computation.1 | async-start | bytes 2359296 | tf_op jit(solution)/shard_map/while/body/eval_jaxpr/all_gather | solution.py:13
  466.6 48.0 %all-reduce.3.cloned.1.call-start = ((), (), s32[]{:S(2)}) async-start(), calls=%async_computation.2 | async-start | bytes 524288 | tf_op jit(solution)/shard_map/while/body/eval_jaxpr/psum | solution.py:117
  466.7 9.3 collective-permute-start
  470.9 106.4 %all-gather.11.cloned.1.call-start = ((), (), s32[]{:S(2)}) async-start(), calls=%async_computation.1 | async-start | bytes 2359296 | tf_op jit(solution)/shard_map/while/body/eval_jaxpr/all_gather | solution.py:13
  579.1 50.3 %all-reduce.3.cloned.1.call-start = ((), (), s32[]{:S(2)}) async-start(), calls=%async_computation.2 | async-start | bytes 524288 | tf_op jit(solution)/shard_map/while/body/eval_jaxpr/psum | solution.py:117
  579.2 9.3 collective-permute-start
  583.4 107.5 %all-gather.11.cloned.1.call-start = ((), (), s32[]{:S(2)}) async-start(), calls=%async_computation.1 | async-start | bytes 2359296 | tf_op jit(solution)/shard_map/while/body/eval_jaxpr/all_gather | solution.py:13
  692.7 49.0 %all-reduce.3.cloned.1.call-start = ((), (), s32[]{:S(2)}) async-start(), calls=%async_computation.2 | async-start | bytes 524288 | tf_op jit(solution)/shard_map/while/body/eval_jaxpr/psum | solution.py:117
  692.8 9.9 collective-permute-start
  702.7 99.0 %all-gather.11.cloned.1.call-start = ((), (), s32[]{:S(2)}) async-start(), calls=%async_computation.1 | async-start | bytes 2359296 | tf_op jit(solution)/shard_map/while/body/eval_jaxpr/all_gather | solution.py:13
  803.4 85.0 %all-reduce.3.cloned.1.call-start = ((), (), s32[]{:S(2)}) async-start(), calls=%async_computation.2 | async-start | bytes 524288 | tf_op jit(solution)/shard_map/while/body/eval_jaxpr/psum | solution.py:117
  803.6 18.9 %collective-permute-start = (f32[512,128]{1,0:T(8,128)S(1)}, f32[512,128]{1,0:T(8,128)S(1)}, u32[]{:S(2)}, u32[]{:S(2)}) collective-permute-start(f32[512,128]{1,0:T(8,128)S(1)} %get-tuple-element.813), channel_id=1, source_target_pairs={{0,24},{8,0},{16,8},{24,16},{1,25},{9,1},{17,9},{25,17},{2,26},{10... | collective-permute-start | bytes 786440 | tf_op jit(solution)/shard_map/while/body/eval_jaxpr/ppermute | solution.py:21
  807.8 104.3 %all-gather.11.cloned.1.call-start = ((), (), s32[]{:S(2)}) async-start(), calls=%async_computation.1 | async-start | bytes 2359296 | tf_op jit(solution)/shard_map/while/body/eval_jaxpr/all_gather | solution.py:13
  913.8 48.0 %all-reduce.3.cloned.1.call-start = ((), (), s32[]{:S(2)}) async-start(), calls=%async_computation.2 | async-start | bytes 524288 | tf_op jit(solution)/shard_map/while/body/eval_jaxpr/psum | solution.py:117
  914.0 9.3 collective-permute-start
  918.1 106.4 %all-gather.11.cloned.1.call-start = ((), (), s32[]{:S(2)}) async-start(), calls=%async_computation.1 | async-start | bytes 2359296 | tf_op jit(solution)/shard_map/while/body/eval_jaxpr/all_gather | solution.py:13
  1026.3 50.3 %all-reduce.3.cloned.1.call-start = ((), (), s32[]{:S(2)}) async-start(), calls=%async_computation.2 | async-start | bytes 524288 | tf_op jit(solution)/shard_map/while/body/eval_jaxpr/psum | solution.py:117
  1026.4 9.3 collective-permute-start
  1030.6 107.5 %all-gather.11.cloned.1.call-start = ((), (), s32[]{:S(2)}) async-start(), calls=%async_computation.1 | async-start | bytes 2359296 | tf_op jit(solution)/shard_map/while/body/eval_jaxpr/all_gather | solution.py:13
  1139.9 49.8 %all-reduce.3.cloned.1.call-start = ((), (), s32[]{:S(2)}) async-start(), calls=%async_computation.2 | async-start | bytes 524288 | tf_op jit(solution)/shard_map/while/body/eval_jaxpr/psum | solution.py:117
  1140.0 9.3 collective-permute-start
  1144.2 105.5 %all-gather.11.cloned.1.call-start = ((), (), s32[]{:S(2)}) async-start(), calls=%async_computation.1 | async-start | bytes 2359296 | tf_op jit(solution)/shard_map/while/body/eval_jaxpr/all_gather | solution.py:13
  1251.4 49.3 %all-reduce.3.cloned.1.call-start = ((), (), s32[]{:S(2)}) async-start(), calls=%async_computation.2 | async-start | bytes 524288 | tf_op jit(solution)/shard_map/while/body/eval_jaxpr/psum | solution.py:117
  1251.6 9.3 collective-permute-start
  1255.8 105.6 %all-gather.11.cloned.1.call-start = ((), (), s32[]{:S(2)}) async-start(), calls=%async_computation.1 | async-start | bytes 2359296 | tf_op jit(solution)/shard_map/while/body/eval_jaxpr/all_gather | solution.py:13
  1363.1 48.0 %all-reduce.3.cloned.1.call-start = ((), (), s32[]{:S(2)}) async-start(), calls=%async_computation.2 | async-start | bytes 524288 | tf_op jit(solution)/shard_map/while/body/eval_jaxpr/psum | solution.py:117
  1363.3 9.3 collective-permute-start
  1367.5 106.4 %all-gather.11.cloned.1.call-start = ((), (), s32[]{:S(2)}) async-start(), calls=%async_computation.1 | async-start | bytes 2359296 | tf_op jit(solution)/shard_map/while/body/eval_jaxpr/all_gather | solution.py:13
  1475.7 50.3 %all-reduce.3.cloned.1.call-start = ((), (), s32[]{:S(2)}) async-start(), calls=%async_computation.2 | async-start | bytes 524288 | tf_op jit(solution)/shard_map/while/body/eval_jaxpr/psum | solution.py:117
  1475.8 9.3 collective-permute-start
  1480.0 107.5 %all-gather.11.cloned.1.call-start = ((), (), s32[]{:S(2)}) async-start(), calls=%async_computation.1 | async-start | bytes 2359296 | tf_op jit(solution)/shard_map/while/body/eval_jaxpr/all_gather | solution.py:13
  1589.3 49.0 %all-reduce.3.cloned.1.call-start = ((), (), s32[]{:S(2)}) async-start(), calls=%async_computation.2 | async-start | bytes 524288 | tf_op jit(solution)/shard_map/while/body/eval_jaxpr/psum | solution.py:117
  1589.4 9.9 collective-permute-start
  1599.3 99.0 %all-gather.11.cloned.1.call-start = ((), (), s32[]{:S(2)}) async-start(), calls=%async_computation.1 | async-start | bytes 2359296 | tf_op jit(solution)/shard_map/while/body/eval_jaxpr/all_gather | solution.py:13
  1700.0 85.0 %all-reduce.3.cloned.1.call-start = ((), (), s32[]{:S(2)}) async-start(), calls=%async_computation.2 | async-start | bytes 524288 | tf_op jit(solution)/shard_map/while/body/eval_jaxpr/psum | solution.py:117
  1700.2 18.9 %collective-permute-start = (f32[512,128]{1,0:T(8,128)S(1)}, f32[512,128]{1,0:T(8,128)S(1)}, u32[]{:S(2)}, u32[]{:S(2)}) collective-permute-start(f32[512,128]{1,0:T(8,128)S(1)} %get-tuple-element.813), channel_id=1, source_target_pairs={{0,24},{8,0},{16,8},{24,16},{1,25},{9,1},{17,9},{25,17},{2,26},{10... | collective-permute-start | bytes 786440 | tf_op jit(solution)/shard_map/while/body/eval_jaxpr/ppermute | solution.py:21
  1710.0 98.6 %all-gather.11.cloned.1.call-start = ((), (), s32[]{:S(2)}) async-start(), calls=%async_computation.1 | async-start | bytes 2359296 | tf_op jit(solution)/shard_map/while/body/eval_jaxpr/all_gather | solution.py:13
  (16 other events, 22.0 us)
Sparse Core Ops, SparseCore 0:
  36.0 91.7 all-gather.8
  134.1 45.8 all-reduce.2
  247.7 45.3 all-reduce.2
  359.3 44.8 all-reduce.2
  471.0 43.5 all-reduce.2
  583.5 45.8 all-reduce.2
  702.8 38.8 all-reduce.2
  807.9 44.0 all-reduce.2
  918.2 43.5 all-reduce.2
  1030.7 45.8 all-reduce.2
  1144.3 45.3 all-reduce.2
  1255.9 44.8 all-reduce.2
  1367.6 43.5 all-reduce.2
  1480.1 45.8 all-reduce.2
  1599.4 38.8 all-reduce.2
  1710.1 44.1 all-reduce.2
Sparse Core Ops, SparseCore 1:
  140.1 101.4 all-gather.10
  253.6 99.4 all-gather.10
  365.2 99.5 all-gather.10
  476.9 100.3 all-gather.10
  589.4 101.4 all-gather.10
  705.9 95.7 all-gather.10
  888.5 23.5 all-gather.10
  924.2 100.3 all-gather.10
  1036.6 101.4 all-gather.10
  1150.2 99.4 all-gather.10
  1261.8 99.5 all-gather.10
  1373.5 100.3 all-gather.10
  1486.0 101.4 all-gather.10
  1602.5 95.7 all-gather.10
  1785.1 23.5 all-gather.10
